TPU v7x, 32 devices: a whole 2x2x4 slice. The times are simulated.
32 devices in a mesh: grp: 4 (over x, core), pages: 8 (over z, y).
Axes of the slice: x: 2, y: 2, z: 4, core: 2. Of those that a mesh axis runs over, the one named last changes fastest.
Arguments:
- queries: bfloat16 [128, 64, 2048], P(('grp', 'pages')), parts along dimension 0, may hold values from -500 to 500
- tree_keys: bfloat16 [128, 64, 512], P(('grp', 'pages')), parts along dimension 0, may hold values from -6 to 6
- tree_values: bfloat16 [128, 64, 512], P(('grp', 'pages')), parts along dimension 0, may hold values from -6 to 6
- page_keys: bfloat16 [256, 256, 512], P(('grp', 'pages')), parts along dimension 0, may hold values from -6 to 6
- page_values: bfloat16 [256, 256, 512], P(('grp', 'pages')), parts along dimension 0, may hold values from -6 to 6
- page_table: int32 [128, 4], P(('grp', 'pages')), parts along dimension 0, may hold values from 0 to 63, as said below
- prefix_lengths: int32 [128], P(('grp', 'pages')), parts along dimension 0, may hold values from 513 to 1024
- tree_parents: int32 [128, 64], P(('grp', 'pages')), parts along dimension 0, may hold values from -1 to 62, as said below
- live_lengths: int32 [128], P(('grp', 'pages')), parts along dimension 0, may hold values from 1 to 64
Outputs:
- attended: bfloat16 [128, 64, 2048], P(('grp', 'pages')), parts along dimension 0
- page_reads: int32 [256], P(('grp', 'pages')), parts along dimension 0
There are 4 independent parts, one for each index of `grp`. A program takes and returns all parts, laid end to end along the dimension named above; each array names one. Nothing has to cross between parts.
Inputs may be any that keep to these rules, and one draw needn't show every extreme that they name: `page_table`: the owner of page p is index p // 8 along pages. Over the rows of one device, the used slots name pages of any one owner at most 2 times, and in every draw each device names some owner exactly 2 times. `tree_parents`: entry t is -1 for t = 0 and a number below t otherwise.
All inputs are finite; a program needn't handle non-finite values.
Results may differ from a plain program's by a relative error of at most 0.0085.
Values may be sent and summed in bfloat16 or wider, within the bound.
A program may use at most 192 MiB of HBM per device.

v0:
```python
import functools

import jax
import jax.numpy as jnp
from jax import lax
from jax.experimental import pallas as pl
from jax.experimental.pallas import tpu as pltpu
from jax.sharding import PartitionSpec as P

QH = 16
KVH = 4
HD = 128
GROUPS = QH // KVH
NEG_BIG = -1e30
SCALE = HD ** (-0.5)
NT = (((1,), (1,)), ((), ()))
MESH = pl.DeviceIdType.MESH


def head(h):
    return slice(h * HD, (h + 1) * HD)


def attend(query_of, keys_of, values_of, allowed, out_to, stats, lane, first):
    for k in range(KVH):
        query = jnp.concatenate([query_of(k * GROUPS + g) for g in range(GROUPS)], axis=0)
        scores = (
            lax.dot_general(query, keys_of(k), NT, preferred_element_type=jnp.float32) * SCALE
        )
        scores = jnp.where(allowed, scores, NEG_BIG)
        peak = jnp.max(scores, axis=-1, keepdims=True)
        expo = jnp.exp(scores - peak)
        total = jnp.sum(expo, axis=-1, keepdims=True)
        out = jnp.dot(
            expo.astype(jnp.bfloat16), values_of(k), preferred_element_type=jnp.float32
        )
        rows = out.shape[0] // GROUPS
        for g in range(GROUPS):
            h = k * GROUPS + g
            part = slice(g * rows, (g + 1) * rows)
            out_to(h, out[part])
            stats = jnp.where(lane == first + h, peak[part], stats)
            stats = jnp.where(lane == first + QH + h, total[part], stats)
    return stats


def exchange(
    n,
    cap,
    table,
    prefix,
    live,
    parents_ref,
    q_ref,
    tk_ref,
    tv_ref,
    pk_hbm,
    pv_hbm,
    attended,
    reads_ref,
    pk_ref,
    pv_ref,
    target,
    used,
    label_ref,
    labels,
    label_now,
    got_out,
    got_stats,
    tree_out,
    tree_stats,
    q_all,
    q_now,
    out_send,
    stats_send,
    label_send_sem,
    label_recv_sem,
    q_send_sem,
    q_recv_sem,
    out_send_sem,
    out_recv_sem,
    stats_send_sem,
    stats_recv_sem,
    local_sem,
):
    reqs, tree, _ = q_ref.shape
    pages_here, page, _ = pk_ref.shape
    slots = table.shape[1]
    lanes = cap * 2 * QH
    fold = HD // lanes
    rows_held = tree // fold
    depth = n // 2
    me = lax.axis_index("pages")
    z, y = me // 2, me % 2
    other = 1 - y
    partner = z * 2 + other

    load_keys = pltpu.make_async_copy(pk_hbm, pk_ref, local_sem.at[2])
    load_values = pltpu.make_async_copy(pv_hbm, pv_ref, local_sem.at[3])
    load_keys.start()
    load_values.start()

    barrier = pltpu.get_barrier_semaphore()

    def greet(i, _):
        pl.semaphore_signal(
            barrier, inc=1, device_id={"pages": (me + i) % n}, device_id_type=MESH
        )
        return 0

    lax.fori_loop(1, n, greet, 0)
    pl.semaphore_wait(barrier, n - 1)

    def q_copy(src_ref, src, i, way, to):
        return pltpu.make_async_remote_copy(
            src_ref=src_ref,
            dst_ref=q_all.at[src, i],
            send_sem=q_send_sem.at[way, src // 2, i],
            recv_sem=q_recv_sem.at[src, i],
            device_id={"pages": to},
            device_id_type=MESH,
        )

    def out_copy(d):
        return pltpu.make_async_remote_copy(
            src_ref=out_send.at[d],
            dst_ref=got_out.at[pl.ds(me * cap, cap)],
            send_sem=out_send_sem.at[d],
            recv_sem=out_recv_sem.at[me],
            device_id={"pages": d},
            device_id_type=MESH,
        )

    def stats_copy(d):
        return pltpu.make_async_remote_copy(
            src_ref=stats_send.at[d],
            dst_ref=got_stats.at[me],
            send_sem=stats_send_sem.at[d],
            recv_sem=stats_recv_sem.at[me],
            device_id={"pages": d},
            device_id_type=MESH,
        )

    def q_arrive(src, i):
        pltpu.make_async_remote_copy(
            src_ref=q_all.at[src, i],
            dst_ref=q_all.at[src, i],
            send_sem=q_send_sem.at[0, src // 2, i],
            recv_sem=q_recv_sem.at[src, i],
            device_id={"pages": partner},
            device_id_type=MESH,
        ).wait_recv()

    for i in range(reqs):
        q_copy(q_ref.at[i], me, i, 2, partner).start()

        @pl.when(z + 1 < depth)
        def _():
            q_copy(q_ref.at[i], me, i, 0, me + 2).start()

        @pl.when(z > 0)
        def _():
            q_copy(q_ref.at[i], me, i, 1, me - 2).start()

    label_row = lax.broadcasted_iota(jnp.int32, (n, HD), 0)
    label_lane = lax.broadcasted_iota(jnp.int32, (n, HD), 1)
    told = jnp.zeros((n, HD), jnp.int32)
    owners, taken = [], []
    for p in range(reqs * slots):
        r, j = p // slots, p % slots
        count = jnp.clip(prefix[r] - j * page, 0, page)
        owner = lax.div(table[r, j], jnp.int32(pages_here))
        rank = jnp.int32(0)
        for earlier in range(p):
            same = (owners[earlier] == owner) & (taken[earlier] > 0)
            rank = rank + jnp.where(same, 1, 0)
        takes = jnp.where(count > 0, 1, 0)
        owners.append(owner)
        taken.append(takes)
        used[p] = takes
        target[p] = jnp.where(count > 0, owner * cap + rank, me * cap)
        row = label_row == jnp.where(count > 0, owner, -1)
        facts = (table[r, j] - owner * pages_here, count, r, live[r])
        for f, fact in enumerate(facts):
            told = jnp.where(row & (label_lane == rank * 4 + f), fact, told)
    for d in range(n):
        label_ref[d, 0:1, :] = told[d : d + 1]

    def label_copy(d):
        return pltpu.make_async_remote_copy(
            src_ref=label_ref.at[d],
            dst_ref=labels.at[me],
            send_sem=label_send_sem.at[d],
            recv_sem=label_recv_sem.at[me],
            device_id={"pages": d},
            device_id_type=MESH,
        )

    def tell(i, _):
        label_copy((me + i) % n).start()
        return 0

    lax.fori_loop(1, n, tell, 0)

    lane = lax.broadcasted_iota(jnp.int32, (tree, HD), 1)
    key_lane = lax.broadcasted_iota(jnp.int32, (GROUPS * tree, page), 1)

    def serve(d):
        stats = jnp.zeros((tree, HD), jnp.float32)
        for c in range(cap):
            which, count, req = (label_now[d, 0, c * 4 + f] for f in range(3))

            def out_to(h, value):
                out_send[d, c, :, head(h)] = value.astype(jnp.bfloat16)

            stats = attend(
                lambda h: q_now[req, :, head(h)],
                lambda k: pk_ref[which, :, head(k)],
                lambda k: pv_ref[which, :, head(k)],
                key_lane < count,
                out_to,
                stats,
                lane,
                c * 2 * QH,
            )
        stats_send[d] = jnp.concatenate(
            [stats[i * rows_held : (i + 1) * rows_held, :lanes] for i in range(fold)], axis=1
        )

    def one_tree(r, _):
        source = lax.broadcasted_iota(jnp.int32, (tree, tree), 0)
        child = lax.broadcasted_iota(jnp.int32, (tree, tree), 1)
        linked = (source == parents_ref[pl.ds(r, 1), :]) | (source == child)
        same = jnp.where(source == child, 1.0, 0.0).astype(jnp.bfloat16)
        reach = jnp.where(linked, 1.0, 0.0).astype(jnp.bfloat16)
        for level in range((tree - 1).bit_length()):
            reach = jnp.where(
                jnp.dot(reach, reach, preferred_element_type=jnp.float32) > 0, 1.0, 0.0
            ).astype(jnp.bfloat16)
        upright = lax.dot_general(
            reach, same, (((0,), (0,)), ((), ())), preferred_element_type=jnp.float32
        )
        open_ = jnp.where(child < live[r], upright, 0.0)
        allowed = jnp.concatenate([open_] * GROUPS, axis=0) > 0

        def out_to(h, value):
            tree_out[r, :, head(h)] = value

        tree_stats[r] = attend(
            lambda h: q_ref[r, :, head(h)],
            lambda k: tk_ref[r, :, head(k)],
            lambda k: tv_ref[r, :, head(k)],
            allowed,
            out_to,
            jnp.zeros((tree, HD), jnp.float32),
            lane,
            0,
        )
        return 0

    lax.fori_loop(0, reqs, one_tree, 0)

    labels[me] = label_ref[me]

    def hear(i, _):
        d = (me + i) % n
        pltpu.make_async_remote_copy(
            src_ref=label_ref.at[d],
            dst_ref=labels.at[d],
            send_sem=label_send_sem.at[d],
            recv_sem=label_recv_sem.at[d],
            device_id={"pages": d},
            device_id_type=MESH,
        ).wait()
        return 0

    lax.fori_loop(1, n, hear, 0)
    into_scalars = pltpu.make_async_copy(labels, label_now, local_sem.at[0])
    into_scalars.start()
    into_scalars.wait()
    load_keys.wait()
    load_values.wait()

    q_now[...] = q_ref[...]
    serve(me)
    for c in range(cap):
        got_out[me * cap + c] = out_send[me, c]
    got_stats[me] = stats_send[me]

    page_row = lax.broadcasted_iota(jnp.int32, (pages_here, HD), 0)

    def count_reads(d, reads):
        for c in range(cap):
            which, count, _, lives = (label_now[d, 0, c * 4 + f] for f in range(4))
            lives = jnp.where(count > 0, lives, 0)
            reads = reads + jnp.where(page_row == which, lives, 0)
        return reads

    reads_ref[...] = lax.fori_loop(
        0, n, count_reads, jnp.zeros((pages_here, HD), jnp.int32)
    )

    def step(s, _):
        for i in range(reqs):

            @pl.when(z - s >= 0)
            def _():
                src = me - 2 * s
                q_arrive(src, i)
                q_copy(q_all.at[src, i], src, i, 2, partner).start()

                @pl.when(z + 1 < depth)
                def _():
                    q_copy(q_all.at[src, i], src, i, 0, me + 2).start()

            @pl.when(z + s < depth)
            def _():
                src = me + 2 * s
                q_arrive(src, i)
                q_copy(q_all.at[src, i], src, i, 2, partner).start()

                @pl.when(z > 0)
                def _():
                    q_copy(q_all.at[src, i], src, i, 1, me - 2).start()

        def case(k, _):
            crossed = k // 2
            far = s - crossed
            row = z + far * (2 * (k % 2) - 1)
            column = y + crossed * (other - y)
            d = row * 2 + column
            valid = (row >= 0) & (row < depth) & ((far > 0) | (k == 2))

            @pl.when(valid)
            def _():
                @pl.when(crossed == 1)
                def _():
                    for i in range(reqs):
                        q_arrive(d, i)

                q_now[...] = q_all[d]
                serve(d)
                out_copy(d).start()
                stats_copy(d).start()

            return 0

        lax.fori_loop(0, 4, case, 0)
        return 0

    lax.fori_loop(1, depth + 1, step, 0)

    def finish(i, _):
        d = (me + i) % n
        out_copy(d).wait_send()
        stats_copy(d).wait_send()
        pltpu.make_async_remote_copy(
            src_ref=out_send.at[d],
            dst_ref=got_out.at[pl.ds(d * cap, cap)],
            send_sem=out_send_sem.at[d],
            recv_sem=out_recv_sem.at[d],
            device_id={"pages": d},
            device_id_type=MESH,
        ).wait_recv()
        pltpu.make_async_remote_copy(
            src_ref=stats_send.at[d],
            dst_ref=got_stats.at[d],
            send_sem=stats_send_sem.at[d],
            recv_sem=stats_recv_sem.at[d],
            device_id={"pages": d},
            device_id_type=MESH,
        ).wait_recv()
        return 0

    lax.fori_loop(1, n, finish, 0)

    def drain(row, _):
        src = row * 2 + y
        for i in range(reqs):
            q_copy(q_all.at[src, i], src, i, 2, partner).wait_send()

            @pl.when((row <= z) & (z + 1 < depth))
            def _():
                q_copy(q_all.at[src, i], src, i, 0, me + 2).wait_send()

            @pl.when((row >= z) & (z > 0))
            def _():
                q_copy(q_all.at[src, i], src, i, 1, me - 2).wait_send()

        return 0

    lax.fori_loop(0, depth, drain, 0)

    def merge(r, _):
        tree_peak, tree_total = tree_stats[r, :, :QH], tree_stats[r, :, QH : 2 * QH]
        top = tree_peak
        peaks, totals = [], []
        for j in range(slots):
            where_ = target[r * slots + j]
            live_slot = used[r * slots + j] > 0
            packed = got_stats[where_ // cap]
            held = jnp.concatenate(
                [packed[:, i * lanes : (i + 1) * lanes] for i in range(fold)], axis=0
            )
            mine = held[:, : 2 * QH]
            for c in range(1, cap):
                mine = jnp.where(
                    where_ % cap == c, held[:, c * 2 * QH : (c + 1) * 2 * QH], mine
                )
            peaks.append(jnp.where(live_slot, mine[:, :QH], NEG_BIG))
            totals.append(mine[:, QH:])
            top = jnp.maximum(top, peaks[j])
        tree_scale = jnp.exp(tree_peak - top)
        scales = [
            jnp.where(used[r * slots + j] > 0, jnp.exp(peaks[j] - top), 0.0)
            for j in range(slots)
        ]
        total = tree_total * tree_scale
        for j in range(slots):
            total = total + scales[j] * totals[j]
        tree_scale = tree_scale / total
        scales = [scale / total for scale in scales]
        for h in range(QH):
            mixed = tree_out[r, :, head(h)] * tree_scale[:, h : h + 1]
            for j in range(slots):
                part = got_out[target[r * slots + j], :, head(h)].astype(jnp.float32)
                mixed = mixed + part * scales[j][:, h : h + 1]
            attended[r, :, head(h)] = mixed.astype(jnp.bfloat16)
        return 0

    lax.fori_loop(0, reqs, merge, 0)


def shards(
    queries,
    tree_keys,
    tree_values,
    page_keys,
    page_values,
    page_table,
    prefix_lengths,
    tree_parents,
    live_lengths,
):
    n = lax.axis_size("pages")
    reqs, tree, width = queries.shape
    pages_here = page_keys.shape[0]
    slots = page_table.shape[1]
    pairs = reqs * slots
    cap = max(1, pairs // n)

    smem = pl.BlockSpec(memory_space=pltpu.SMEM)
    vmem = pl.BlockSpec(memory_space=pltpu.VMEM)
    hbm = pl.BlockSpec(memory_space=pl.ANY)
    depth = n // 2
    held_stats = (n, tree * cap * 2 * QH // HD, HD)
    attended, reads = pl.pallas_call(
        functools.partial(exchange, n, cap),
        out_shape=(
            jax.ShapeDtypeStruct((reqs, tree, width), jnp.bfloat16),
            jax.ShapeDtypeStruct((pages_here, HD), jnp.int32),
        ),
        in_specs=[smem] * 3 + [vmem] * 4 + [hbm] * 2,
        out_specs=(vmem, vmem),
        scratch_shapes=[
            pltpu.VMEM(page_keys.shape, jnp.bfloat16),
            pltpu.VMEM(page_values.shape, jnp.bfloat16),
            pltpu.SMEM((pairs,), jnp.int32),
            pltpu.SMEM((pairs,), jnp.int32),
            pltpu.VMEM((n, 8, HD), jnp.int32),
            pltpu.VMEM((n, 8, HD), jnp.int32),
            pltpu.SMEM((n, 8, HD), jnp.int32),
            pltpu.VMEM((n * cap, tree, width), jnp.bfloat16),
            pltpu.VMEM(held_stats, jnp.float32),
            pltpu.VMEM((reqs, tree, width), jnp.float32),
            pltpu.VMEM((reqs, tree, HD), jnp.float32),
            pltpu.VMEM((n, reqs, tree, width), jnp.bfloat16),
            pltpu.VMEM((reqs, tree, width), jnp.bfloat16),
            pltpu.VMEM((n, cap, tree, width), jnp.bfloat16),
            pltpu.VMEM(held_stats, jnp.float32),
            pltpu.SemaphoreType.DMA((n,)),
            pltpu.SemaphoreType.DMA((n,)),
            pltpu.SemaphoreType.DMA((3, depth, reqs)),
            pltpu.SemaphoreType.DMA((n, reqs)),
            pltpu.SemaphoreType.DMA((n,)),
            pltpu.SemaphoreType.DMA((n,)),
            pltpu.SemaphoreType.DMA((n,)),
            pltpu.SemaphoreType.DMA((n,)),
            pltpu.SemaphoreType.DMA((4,)),
        ],
        compiler_params=pltpu.CompilerParams(
            collective_id=0, has_side_effects=True, vmem_limit_bytes=63 * 1024 * 1024
        ),
        name="exchange",
    )(
        page_table,
        prefix_lengths,
        live_lengths,
        tree_parents,
        queries,
        tree_keys,
        tree_values,
        page_keys,
        page_values,
    )
    return (attended, reads[:, 0])


def solution(mesh):
    rows = P(("grp", "pages"), None, None)
    return jax.shard_map(
        shards,
        mesh=mesh,
        in_specs=(
            rows,
            rows,
            rows,
            rows,
            rows,
            P(("grp", "pages"), None),
            P(("grp", "pages")),
            P(("grp", "pages"), None),
            P(("grp", "pages")),
        ),
        out_specs=(rows, P(("grp", "pages"))),
        check_vma=False,
    )
```

profile of v0, /device:TPU:0, one launch (start us, length us, event | category | flops | bytes accessed | tf_op | source)
XLA Modules:
  0.0 173.9 jit_solution(9322006604113363124)
XLA Ops:
  0.6 169.7 %exchange.1 = (bf16[4,64,2048]{2,1,0:T(8,128)(2,1)}, s32[8,128]{1,0:T(8,128)}) custom-call(s32[4,4]{1,0:T(4,128)} %table.1, s32[4]{0:T(128)} %prefix.1, s32[4]{0:T(128)} %live.1, s32[4,64]{1,0:T(4,128)} %parents_ref.1, bf16[4,64,2048]{2,1,0:T(8,128)(2,1)} %q_ref.1, bf16[4,64,512]{2,1,0:T(8,128)(2,1)} %tk_ref.1, bf16[4,64,512]{2,1,0:T(8,128)(2,1)} %tv_ref.1, ...), custom_call_target="tpu_custom_call" | custom-call | tf_op jit(solution)/shard_map/exchange/pallas_call | solution.py:457
  170.3 1.3 slice_reduce_fusion
  171.6 2.3 %copy.12 = bf16[4,64,2048]{2,1,0:T(8,128)(2,1)} copy(bf16[4,64,2048]{2,1,0:T(8,128)(2,1)} %get-tuple-element.8) | data formatting | bytes 2097152
where the time goes:
time: 174 us
  Pallas kernels  170 us (98%)
  local copies, waits for them, and re-layouts  3.6 us (2%)
    pallas_call x1, Pallas kernels, shards(): pl.pallas_call(functools.partial(exchange, n, cap), out_shape=(jax.ShapeD...  170 us

commit v1 on v0

--- a/solution.py
+++ b/solution.py
@@ -1,4 +1,6 @@
 import functools
+import heapq
+import itertools
 
 import jax
 import jax.numpy as jnp
@@ -14,11 +16,730 @@
 NEG_BIG = -1e30
 SCALE = HD ** (-0.5)
 NT = (((1,), (1,)), ((), ()))
+TN = (((0,), (0,)), ((), ()))
 MESH = pl.DeviceIdType.MESH
+CHUNKS = 4
+GRANT = 63 * 1024 * 1024
+
+PICK, LOCAL, ACROSS, MERGE, Q_RIGHT, Q_LEFT, STATE, Y_QUERY, Y_PART = range(9)
 
 
 def head(h):
     return slice(h * HD, (h + 1) * HD)
+
+
+def plan(depth, chunks, start=5.0):
+    per = 4.0 / chunks
+    wire = {Q_RIGHT: 5.63 * per, Q_LEFT: 5.63 * per, STATE: 5.8 * per}
+    wire.update({Y_QUERY: 2.82 * per, Y_PART: 2.9 * per})
+    work = {PICK: 0.15 * per, LOCAL: 0.6 * per, ACROSS: 0.6 * per, MERGE: 0.45 * per}
+    delay = 1.8
+    rank = {PICK: 0, ACROSS: 1, MERGE: 2, LOCAL: 3}
+    events, tick = [], itertools.count()
+    have = [set() for _ in range(depth)]
+    queue, busy, last = {}, {}, {}
+    idle = [False] * depth
+    todo = [
+        {(kind, s, k) for kind in rank for s in range(depth) for k in range(chunks)}
+        for _ in range(depth)
+    ]
+    issued = [[] for _ in range(depth)]
+
+    def post(time, what, *facts):
+        heapq.heappush(events, (time, next(tick), what, facts))
+
+    def pump(time, key):
+        if busy.get(key) or not queue.get(key):
+            return
+        _, _, ready, op, tag, dest = heapq.heappop(queue[key])
+        busy[key] = True
+        issued[key[0]].append((max(ready, last.get(key, 0.0)), 0, next(tick), op))
+        last[key] = time
+        post(time + wire[op[0]], "free", key)
+        post(time + wire[op[0]] + delay, "land", tag, dest)
+
+    def send(time, z, link, op, tag, dest):
+        order = (op[0] not in (Q_RIGHT, Q_LEFT, Y_QUERY), -abs(op[1] - z), op[2])
+        heapq.heappush(
+            queue.setdefault((z, link), []), (order, next(tick), time, op, tag, dest)
+        )
+        pump(time, (z, link))
+
+    def send_query(time, z, s, k):
+        if s <= z < depth - 1:
+            send(time, z, "right", (Q_RIGHT, s, k), ("q", s, k), z + 1)
+        if s >= z > 0:
+            send(time, z, "left", (Q_LEFT, s, k), ("q", s, k), z - 1)
+
+    def ready(z, op):
+        kind, s, k = op
+        if kind == PICK:
+            return s == z or ("q", s, k) in have[z]
+        if kind == LOCAL:
+            return (PICK, s, k) in have[z]
+        if kind == ACROSS:
+            return ("yq", s, k) in have[z]
+        need = [(LOCAL, s, k), ("yp", s, k)]
+        need += [("right", s, k)] * (s >= z and z > 0)
+        need += [("left", s, k)] * (s <= z and z < depth - 1)
+        return all(n in have[z] for n in need)
+
+    def turn(time, z):
+        if not idle[z]:
+            return
+        able = [op for op in todo[z] if ready(z, op)]
+        if not able:
+            return
+        op = min(able, key=lambda o: (rank[o[0]], -abs(o[1] - z), o[2], o[1]))
+        todo[z].remove(op)
+        issued[z].append((time, 1, next(tick), op))
+        idle[z] = False
+        if op[0] == PICK and op[1] != z:
+            send_query(time + 1e-3, z, op[1], op[2])
+        post(time + work[op[0]], "done", z, op)
+
+    for z in range(depth):
+        for k in range(chunks):
+            send_query(0.0, z, z, k)
+        post(start, "done", z, None)
+    while events:
+        time, _, what, facts = heapq.heappop(events)
+        if what == "free":
+            busy[facts[0]] = False
+            pump(time, facts[0])
+        elif what == "land":
+            have[facts[1]].add(facts[0])
+            turn(time, facts[1])
+        else:
+            z, op = facts
+            idle[z] = True
+            if op is not None:
+                kind, s, k = op
+                have[z].add(op)
+                if kind == PICK:
+                    send(time, z, "y", (Y_QUERY, s, k), ("yq", s, k), z)
+                elif kind == ACROSS:
+                    send(time, z, "y", (Y_PART, s, k), ("yp", s, k), z)
+                elif kind == MERGE and s > z:
+                    send(time, z, "right", (STATE, s, k), ("right", s, k), z + 1)
+                elif kind == MERGE and s < z:
+                    send(time, z, "left", (STATE, s, k), ("left", s, k), z - 1)
+            turn(time, z)
+    items = depth * chunks
+    orders = [
+        [op[0] * items + op[1] * chunks + op[2] for _, _, _, op in sorted(steps)]
+        for steps in issued
+    ]
+    longest = max(len(o) for o in orders)
+    return [o + [-1] * (longest - len(o)) for o in orders]
+
+
+def attend_part(query, keys, values, allowed):
+    scores = lax.dot_general(keys, query, NT, preferred_element_type=jnp.float32) * SCALE
+    scores = jnp.where(allowed, scores, NEG_BIG)
+    peak = jnp.max(scores, axis=0, keepdims=True)
+    expo = jnp.exp(scores - peak)
+    total = jnp.sum(expo, axis=0, keepdims=True)
+    out = lax.dot_general(
+        values, expo.astype(jnp.bfloat16), TN, preferred_element_type=jnp.float32
+    )
+    return out * (1.0 / total), peak + jnp.log(total)
+
+
+def chain(
+    n,
+    cap,
+    chunks,
+    orders,
+    table,
+    prefix,
+    live,
+    parents_ref,
+    tk_ref,
+    tv_ref,
+    q_hbm,
+    pk_hbm,
+    pv_hbm,
+    attended,
+    reads_ref,
+    pk_ref,
+    pv_ref,
+    label_ref,
+    labels,
+    label_now,
+    qa,
+    q_now,
+    yq_send,
+    yq_got,
+    yo_send,
+    yo_got,
+    ys_send,
+    ys_got,
+    loc_o,
+    loc_s,
+    st_o,
+    st_s,
+    tree_o,
+    tree_s,
+    open_ref,
+    label_send_sem,
+    label_recv_sem,
+    q_send_sem,
+    q_recv_sem,
+    yq_send_sem,
+    yq_recv_sem,
+    yo_send_sem,
+    yo_recv_sem,
+    ys_send_sem,
+    ys_recv_sem,
+    so_send_sem,
+    so_recv_sem,
+    ss_send_sem,
+    ss_recv_sem,
+    local_sem,
+):
+    reqs, tree, wide = q_now.shape
+    _, pages_here, page, _ = pk_ref.shape
+    slots = table.shape[1]
+    depth = n // 2
+    items = depth * chunks
+    heads = wide // HD
+    cols = heads * tree
+    tiles = cols // HD
+    me = lax.axis_index("pages")
+    z, y = me // 2, me % 2
+    partner = z * 2 + (1 - y)
+    absent = items + chunks
+
+    loads = []
+    for k in range(chunks):
+        loads.append(
+            pltpu.make_async_copy(
+                q_hbm.at[:, :, pl.ds(k * wide, wide)],
+                qa.at[z * chunks + k],
+                local_sem.at[1 + k],
+            )
+        )
+    page_loads = []
+    for k in range(KVH):
+        for f, (src, dst) in enumerate(((pk_hbm, pk_ref), (pv_hbm, pv_ref))):
+            page_loads.append(
+                pltpu.make_async_copy(
+                    src.at[:, :, pl.ds(k * HD, HD)],
+                    dst.at[k],
+                    local_sem.at[1 + chunks + 2 * k + f],
+                )
+            )
+    for copy in loads + page_loads:
+        copy.start()
+
+    barrier = pltpu.get_barrier_semaphore()
+
+    def greet(i, _):
+        pl.semaphore_signal(
+            barrier, inc=1, device_id={"pages": (me + i) % n}, device_id_type=MESH
+        )
+        return 0
+
+    lax.fori_loop(1, n, greet, 0)
+
+    label_row = lax.broadcasted_iota(jnp.int32, (n, HD), 0)
+    label_lane = lax.broadcasted_iota(jnp.int32, (n, HD), 1)
+    told = jnp.zeros((n, HD), jnp.int32)
+    owners, taken = [], []
+    for p in range(reqs * slots):
+        r, j = p // slots, p % slots
+        count = jnp.clip(prefix[r] - j * page, 0, page)
+        owner = lax.div(table[r, j], jnp.int32(pages_here))
+        rank = jnp.int32(0)
+        for earlier in range(p):
+            same = (owners[earlier] == owner) & (taken[earlier] > 0)
+            rank = rank + jnp.where(same, 1, 0)
+        owners.append(owner)
+        taken.append(jnp.where(count > 0, 1, 0))
+        row = label_row == jnp.where(count > 0, owner, -1)
+        facts = (table[r, j] - owner * pages_here, count, r, live[r])
+        for f, fact in enumerate(facts):
+            told = jnp.where(row & (label_lane == rank * 4 + f), fact, told)
+    for d in range(depth):
+        label_ref[d, 0:2, :] = told[2 * d : 2 * d + 2]
+
+    base, per_word = 9 * items + 1, 3
+    steps = len(orders[0])
+    words = []
+    for first in range(0, steps, per_word):
+        packed = [
+            sum((c + 1) * base**b for b, c in enumerate(o[first : first + per_word]))
+            for o in orders
+        ]
+        word = jnp.int32(packed[0])
+        for row in range(1, depth):
+            if packed[row] != packed[0]:
+                word = jnp.where(z == row, packed[row], word)
+        words.append(word)
+
+    def code_at(i):
+        at, b = i // per_word, i % per_word
+        word = words[0]
+        for w in range(1, len(words)):
+            word = jnp.where(at == w, words[w], word)
+        power = jnp.where(b == 0, 1, jnp.where(b == 1, base, base * base))
+        return (word // power) % base - 1
+
+    pl.semaphore_wait(barrier, n - 1)
+
+    def label_copy(d):
+        return pltpu.make_async_remote_copy(
+            src_ref=label_ref.at[d // 2],
+            dst_ref=labels.at[me],
+            send_sem=label_send_sem.at[d],
+            recv_sem=label_recv_sem.at[me],
+            device_id={"pages": d},
+            device_id_type=MESH,
+        )
+
+    def tell(i, _):
+        label_copy((me + i) % n).start()
+        return 0
+
+    lax.fori_loop(1, n, tell, 0)
+
+    def q_copy(j, way):
+        return pltpu.make_async_remote_copy(
+            src_ref=qa.at[j],
+            dst_ref=qa.at[j],
+            send_sem=q_send_sem.at[way, j],
+            recv_sem=q_recv_sem.at[j],
+            device_id={"pages": me + 2 - 4 * way},
+            device_id_type=MESH,
+        )
+
+    def across(src, dst, send_sem, recv_sem, j):
+        return pltpu.make_async_remote_copy(
+            src_ref=src.at[j],
+            dst_ref=dst.at[j],
+            send_sem=send_sem.at[j],
+            recv_sem=recv_sem.at[j],
+            device_id={"pages": partner},
+            device_id_type=MESH,
+        )
+
+    def yq_copy(j):
+        return across(yq_send, yq_got, yq_send_sem, yq_recv_sem, j)
+
+    def yo_copy(j):
+        return across(yo_send, yo_got, yo_send_sem, yo_recv_sem, j)
+
+    def ys_copy(j):
+        return across(ys_send, ys_got, ys_send_sem, ys_recv_sem, j)
+
+    def state_copies(j, row, k):
+        left = jnp.where(row < z, 1, 0)
+        ends = left * jnp.where(row == z - 1, 1, 0)
+        slot = j + ends * (items - row * chunks)
+        to = {"pages": me + 2 - 4 * left}
+        return (
+            pltpu.make_async_remote_copy(
+                src_ref=st_o.at[j],
+                dst_ref=st_o.at[slot],
+                send_sem=so_send_sem.at[j],
+                recv_sem=so_recv_sem.at[slot],
+                device_id=to,
+                device_id_type=MESH,
+            ),
+            pltpu.make_async_remote_copy(
+                src_ref=st_s.at[j],
+                dst_ref=st_s.at[slot],
+                send_sem=ss_send_sem.at[j],
+                recv_sem=ss_recv_sem.at[slot],
+                device_id=to,
+                device_id_type=MESH,
+            ),
+        )
+
+    def state_arrive(slot):
+        for ref, sem in ((st_o, so_recv_sem), (st_s, ss_recv_sem)):
+            pltpu.make_async_remote_copy(
+                src_ref=ref.at[slot],
+                dst_ref=ref.at[slot],
+                send_sem=sem.at[slot],
+                recv_sem=sem.at[slot],
+                device_id={"pages": partner},
+                device_id_type=MESH,
+            ).wait_recv()
+
+    for copy in loads:
+        copy.wait()
+
+    st_o[absent] = jnp.zeros_like(st_o[absent])
+    st_s[absent] = jnp.full(st_s.shape[1:], NEG_BIG, jnp.float32)
+
+    def q_step(i, _):
+        code = code_at(i)
+        kind, j = code // items, code % items
+
+        @pl.when(kind == Q_RIGHT)
+        def _():
+            q_copy(j, 0).start()
+
+        @pl.when(kind == Q_LEFT)
+        def _():
+            q_copy(j, 1).start()
+
+        return 0
+
+    early = 0
+    while all(o[early] // items in (Q_RIGHT, Q_LEFT) for o in orders):
+        early += 1
+    lax.fori_loop(0, early, q_step, 0)
+
+    def rows_of(query):
+        return jnp.concatenate([query[:, head(h)] for h in range(heads)], axis=0)
+
+    def put_row(ref, index, first, vector):
+        for i in range(tiles):
+            ref[index, first + i : first + i + 1, :] = vector[:, head(i)]
+
+    def get_row(tile, first):
+        return jnp.concatenate(
+            [tile[first + i : first + i + 1, :] for i in range(tiles)], axis=1
+        )
+
+    source = lax.broadcasted_iota(jnp.int32, (tree, tree), 0)
+    child = lax.broadcasted_iota(jnp.int32, (tree, tree), 1)
+    reaches = []
+    for r in range(reqs):
+        linked = (source == parents_ref[r : r + 1, :]) | (source == child)
+        reaches.append(jnp.where(linked, 1.0, 0.0).astype(jnp.bfloat16))
+    for level in range((tree - 1).bit_length()):
+        reaches = [
+            jnp.where(
+                jnp.dot(reach, reach, preferred_element_type=jnp.float32) > 0, 1.0, 0.0
+            ).astype(jnp.bfloat16)
+            for reach in reaches
+        ]
+    for r in range(reqs):
+        open_ = jnp.where(source < live[r], reaches[r].astype(jnp.float32), 0.0)
+        open_ref[r] = jnp.concatenate([open_] * heads, axis=1)
+
+    def tree_step(k, _):
+        kv = k * heads // GROUPS
+        lanes = pl.ds(pl.multiple_of(kv * HD, HD), HD)
+        for r in range(reqs):
+            out, lse = attend_part(
+                rows_of(qa[z * chunks + k, r]),
+                tk_ref[r, :, lanes],
+                tv_ref[r, :, lanes],
+                open_ref[r] > 0,
+            )
+            tree_o[k, r] = out
+            put_row(tree_s, k, r * tiles, lse)
+        return 0
+
+    lax.fori_loop(0, chunks, tree_step, 0)
+
+    labels[me] = label_ref[z]
+
+    def hear(i, _):
+        d = (me + i) % n
+        pltpu.make_async_remote_copy(
+            src_ref=label_ref.at[d // 2],
+            dst_ref=labels.at[d],
+            send_sem=label_send_sem.at[d],
+            recv_sem=label_recv_sem.at[d],
+            device_id={"pages": d},
+            device_id_type=MESH,
+        ).wait()
+        return 0
+
+    lax.fori_loop(1, n, hear, 0)
+    into_scalars = pltpu.make_async_copy(labels, label_now, local_sem.at[0])
+    into_scalars.start()
+    into_scalars.wait()
+    for copy in page_loads:
+        copy.wait()
+
+    key_row = lax.broadcasted_iota(jnp.int32, (page, cols), 0)
+
+    def serve(d, k, query_of, out_ref, stat_ref, j):
+        kv = k * heads // GROUPS
+        for c in range(cap):
+            which, count, req = (label_now[d, y, c * 4 + f] for f in range(3))
+            out, lse = attend_part(
+                rows_of(query_of(c, req)),
+                pk_ref[kv, which],
+                pv_ref[kv, which],
+                key_row < count,
+            )
+            out_ref[j, c] = out.astype(jnp.bfloat16)
+            put_row(stat_ref, j, c * tiles, lse)
+
+    def pick(j, row, k):
+        @pl.when(row != z)
+        def _():
+            pltpu.make_async_remote_copy(
+                src_ref=qa.at[j],
+                dst_ref=qa.at[j],
+                send_sem=q_send_sem.at[0, j],
+                recv_sem=q_recv_sem.at[j],
+                device_id={"pages": partner},
+                device_id_type=MESH,
+            ).wait_recv()
+
+        q_now[...] = qa[j]
+        for c in range(cap):
+            yq_send[j, c] = q_now[label_now[row * 2 + y, 1 - y, c * 4 + 2]]
+
+    def local(j, row, k):
+        q_now[...] = qa[j]
+        serve(row * 2 + y, k, lambda c, req: q_now[req], loc_o, loc_s, j)
+
+    def from_partner(j, row, k):
+        yq_copy(j).wait_recv()
+        serve(row * 2 + (1 - y), k, lambda c, req: yq_got[j, c], yo_send, ys_send, j)
+
+    def merged(j, row, r, others):
+        parts, weights = [], []
+        for held_o, held_s, owner in ((loc_o, loc_s, y), (yo_got, ys_got, 1 - y)):
+            tile = held_s[j]
+            for c in range(cap):
+                count, req = (label_now[row * 2 + y, owner, c * 4 + f] for f in (1, 2))
+                mine = (count > 0) & (req == r)
+                parts.append(held_o[j, c].astype(jnp.float32))
+                weights.append(jnp.where(mine, get_row(tile, c * tiles), NEG_BIG))
+        for part, lse in others:
+            parts.append(part)
+            weights.append(lse)
+        top = functools.reduce(jnp.maximum, weights)
+        weights = [jnp.exp(w - top) for w in weights]
+        total = functools.reduce(jnp.add, weights)
+        rest = 1.0 / total
+        out = parts[0] * (weights[0] * rest)
+        for part, weight in zip(parts[1:], weights[1:]):
+            out = out + part * (weight * rest)
+        return out, top + jnp.log(total)
+
+    def state_part(slot, r):
+        return st_o[slot, r].astype(jnp.float32), get_row(st_s[slot], r * tiles)
+
+    def merge(j, row, k):
+        yo_copy(j).wait_recv()
+        ys_copy(j).wait_recv()
+
+        @pl.when(row != z)
+        def _():
+            comes = jnp.where(
+                row > z, jnp.where(z > 0, 1, 0), jnp.where(z < depth - 1, 1, 0)
+            )
+            slot = absent + comes * (j - absent)
+
+            @pl.when(comes == 1)
+            def _():
+                state_arrive(j)
+
+            for r in range(reqs):
+                out, lse = merged(j, row, r, [state_part(slot, r)])
+                st_o[j, r] = out.astype(jnp.bfloat16)
+                put_row(st_s, j, r * tiles, lse)
+
+        @pl.when(row == z)
+        def _():
+            right = absent + jnp.where(z > 0, 1, 0) * (j - absent)
+            left = absent + jnp.where(z < depth - 1, 1, 0) * (items + k - absent)
+
+            @pl.when(z > 0)
+            def _():
+                state_arrive(j)
+
+            @pl.when(z < depth - 1)
+            def _():
+                state_arrive(items + k)
+
+            for r in range(reqs):
+                own = tree_o[k, r], get_row(tree_s[k], r * tiles)
+                out, _ = merged(
+                    j, row, r, [state_part(right, r), state_part(left, r), own]
+                )
+                upright = out.T.astype(jnp.bfloat16)
+                for h in range(heads):
+                    lanes = pl.ds(pl.multiple_of(k * wide + h * HD, HD), HD)
+                    attended[r, :, lanes] = upright[h * tree : (h + 1) * tree]
+
+    def step(i, _):
+        code = code_at(i)
+        kind, j = code // items, code % items
+        row, k = j // chunks, j % chunks
+
+        @pl.when((kind >= 0) & (kind < Q_RIGHT))
+        def _():
+            @pl.when(kind < ACROSS)
+            def _():
+                @pl.when(kind == PICK)
+                def _():
+                    pick(j, row, k)
+
+                @pl.when(kind == LOCAL)
+                def _():
+                    local(j, row, k)
+
+            @pl.when(kind >= ACROSS)
+            def _():
+                @pl.when(kind == ACROSS)
+                def _():
+                    from_partner(j, row, k)
+
+                @pl.when(kind == MERGE)
+                def _():
+                    merge(j, row, k)
+
+        @pl.when(kind >= Q_RIGHT)
+        def _():
+            @pl.when(kind < STATE)
+            def _():
+                @pl.when(kind == Q_RIGHT)
+                def _():
+                    q_copy(j, 0).start()
+
+                @pl.when(kind == Q_LEFT)
+                def _():
+                    q_copy(j, 1).start()
+
+            @pl.when(kind == STATE)
+            def _():
+                for copy in state_copies(j, row, k):
+                    copy.start()
+
+            @pl.when(kind == Y_QUERY)
+            def _():
+                yq_copy(j).start()
+
+            @pl.when(kind == Y_PART)
+            def _():
+                yo_copy(j).start()
+                ys_copy(j).start()
+
+        return 0
+
+    lax.fori_loop(early, len(orders[0]), step, 0)
+
+    page_row = lax.broadcasted_iota(jnp.int32, (pages_here, HD), 0)
+
+    def count_reads(d, reads):
+        for c in range(cap):
+            which, count, _, lives = (label_now[d, y, c * 4 + f] for f in range(4))
+            lives = jnp.where(count > 0, lives, 0)
+            reads = reads + jnp.where(page_row == which, lives, 0)
+        return reads
+
+    reads_ref[...] = lax.fori_loop(
+        0, n, count_reads, jnp.zeros((pages_here, HD), jnp.int32)
+    )
+
+    def drain(j, _):
+        row, k = j // chunks, j % chunks
+        yq_copy(j).wait_send()
+        yo_copy(j).wait_send()
+        ys_copy(j).wait_send()
+
+        @pl.when((row <= z) & (z < depth - 1))
+        def _():
+            q_copy(j, 0).wait_send()
+
+        @pl.when((row >= z) & (z > 0))
+        def _():
+            q_copy(j, 1).wait_send()
+
+        @pl.when(row != z)
+        def _():
+            for copy in state_copies(j, row, k):
+                copy.wait_send()
+
+        return 0
+
+    lax.fori_loop(0, items, drain, 0)
+
+
+def chain_call(n, cap, args):
+    queries, tree_keys, tree_values, page_keys, page_values = args[:5]
+    page_table, prefix_lengths, tree_parents, live_lengths = args[5:]
+    reqs, tree, width = queries.shape
+    pages_here, page, _ = page_keys.shape
+    chunks, depth = CHUNKS, n // 2
+    items = depth * chunks
+    wide = width // chunks
+    cols = wide // HD * tree
+    tall = max(8, max(reqs, cap) * cols // HD)
+    bf16, f32 = jnp.bfloat16, jnp.float32
+    dma = pltpu.SemaphoreType.DMA
+    smem = pl.BlockSpec(memory_space=pltpu.SMEM)
+    vmem = pl.BlockSpec(memory_space=pltpu.VMEM)
+    hbm = pl.BlockSpec(memory_space=pl.ANY)
+    orders = plan(depth, chunks)
+    vmem_scratch = [
+        ((KVH, pages_here, page, HD), bf16),
+        ((KVH, pages_here, page, HD), bf16),
+        ((depth, 8, HD), jnp.int32),
+        ((n, 8, HD), jnp.int32),
+        None,
+        ((items, reqs, tree, wide), bf16),
+        ((reqs, tree, wide), bf16),
+        ((items, cap, tree, wide), bf16),
+        ((items, cap, tree, wide), bf16),
+        ((items, cap, HD, cols), bf16),
+        ((items, cap, HD, cols), bf16),
+        ((items, tall, HD), f32),
+        ((items, tall, HD), f32),
+        ((items, cap, HD, cols), bf16),
+        ((items, tall, HD), f32),
+        ((items + chunks + 1, reqs, HD, cols), bf16),
+        ((items + chunks + 1, tall, HD), f32),
+        ((chunks, reqs, HD, cols), f32),
+        ((chunks, tall, HD), f32),
+        ((reqs, tree, cols), f32),
+    ]
+    scratch = [s and pltpu.VMEM(*s) for s in vmem_scratch]
+    scratch[4] = pltpu.SMEM((n, 8, HD), jnp.int32)
+    sems = [
+        dma((n,)),
+        dma((n,)),
+        dma((2, items)),
+        dma((items,)),
+        dma((items,)),
+        dma((items,)),
+        dma((items,)),
+        dma((items,)),
+        dma((items,)),
+        dma((items,)),
+        dma((items,)),
+        dma((items + chunks,)),
+        dma((items,)),
+        dma((items + chunks,)),
+        dma((1 + chunks + 2 * KVH,)),
+    ]
+    return pl.pallas_call(
+        functools.partial(chain, n, cap, chunks, orders),
+        out_shape=(
+            jax.ShapeDtypeStruct((reqs, tree, width), bf16),
+            jax.ShapeDtypeStruct((pages_here, HD), jnp.int32),
+        ),
+        in_specs=[smem] * 3 + [vmem] * 3 + [hbm] * 3,
+        out_specs=(vmem, vmem),
+        scratch_shapes=scratch + sems,
+        compiler_params=pltpu.CompilerParams(
+            collective_id=0, has_side_effects=True, vmem_limit_bytes=GRANT
+        ),
+        name="chain",
+    )(
+        page_table,
+        prefix_lengths,
+        live_lengths,
+        tree_parents,
+        tree_keys,
+        tree_values,
+        queries,
+        page_keys,
+        page_values,
+    )
 
 
 def attend(query_of, keys_of, values_of, allowed, out_to, stats, lane, first):
@@ -448,6 +1169,11 @@
     slots = page_table.shape[1]
     pairs = reqs * slots
     cap = max(1, pairs // n)
+    args = (queries, tree_keys, tree_values, page_keys, page_values)
+    args += (page_table, prefix_lengths, tree_parents, live_lengths)
+    if 7 * n * reqs * tree * width < GRANT:
+        attended, reads = chain_call(n, cap, args)
+        return attended, reads[:, 0]
 
     smem = pl.BlockSpec(memory_space=pltpu.SMEM)
     vmem = pl.BlockSpec(memory_space=pltpu.VMEM)

time: 174 us -> 115 us (0.66)
  Pallas kernels: 170 us -> 110 us
    pallas_call x1, Pallas kernels: 170 us -> 110 us  [chain_call(): pl.pallas_call(functools.partial(chain, n, cap, chunks, orders), out_shap...]
where the time goes in v1:
time: 115 us
  Pallas kernels  110 us (96%)
  local copies, waits for them, and re-layouts  3.6 us (3%)
    pallas_call x1, Pallas kernels, chain_call(): pl.pallas_call(functools.partial(chain, n, cap, chunks, orders), out_shap...  110 us
    unnamed x1, local copies, waits for them, and re-layouts  2.3 us

profile of v1, /device:TPU:0, one launch (start us, length us, event | category | flops | bytes accessed | tf_op | source)
XLA Modules:
  0.0 114.5 jit_solution(6574317735768614536)
XLA Ops:
  0.6 110.3 %chain.1 = (bf16[4,64,2048]{2,1,0:T(8,128)(2,1)}, s32[8,128]{1,0:T(8,128)}) custom-call(s32[4,4]{1,0:T(4,128)} %table.1, s32[4]{0:T(128)} %prefix.1, s32[4]{0:T(128)} %live.1, s32[4,64]{1,0:T(4,128)} %parents_ref.1, bf16[4,64,512]{2,1,0:T(8,128)(2,1)} %tk_ref.1, bf16[4,64,512]{2,1,0:T(8,128)(2,1)} %tv_ref.1, bf16[4,64,2048]{2,1,0:T(8,128)(2,1)} %q_hbm.1, ...), custom_call_target="tpu_custom_call" | custom-call | tf_op jit(solution)/shard_map/chain/pallas_call | solution.py:719
  110.9 1.3 %slice_reduce_fusion = s32[8]{0:T(128)} fusion(s32[8,128]{1,0:T(8,128)} %get-tuple-element.5), kind=kLoop, calls=%fused_computation | loop fusion | bytes 64 | tf_op jit(solution)/shard_map/slice | solution.py:1176
  112.2 2.3 %copy.12 = bf16[4,64,2048]{2,1,0:T(8,128)(2,1)} copy(bf16[4,64,2048]{2,1,0:T(8,128)(2,1)} %get-tuple-element.8) | data formatting | bytes 2097152

commit v2 on v1

--- a/solution.py
+++ b/solution.py
@@ -15,33 +15,50 @@
 GROUPS = QH // KVH
 NEG_BIG = -1e30
 SCALE = HD ** (-0.5)
+LOG2E = 1.4426950408889634
 NT = (((1,), (1,)), ((), ()))
 TN = (((0,), (0,)), ((), ()))
 MESH = pl.DeviceIdType.MESH
 CHUNKS = 4
+EARLY = 2
+EARLY_Y = 2
 GRANT = 63 * 1024 * 1024
 
 PICK, LOCAL, ACROSS, MERGE, Q_RIGHT, Q_LEFT, STATE, Y_QUERY, Y_PART = range(9)
+
+
+def split(value, size):
+    if size & (size - 1):
+        return value // size, value % size
+    return value >> (size.bit_length() - 1), value & (size - 1)
 
 
 def head(h):
     return slice(h * HD, (h + 1) * HD)
 
 
-def plan(depth, chunks, start=5.0):
+WEIGHTS = ((40, 20, 0.5), (100, 15, 0.0), (20, 5, 5.0), (40, 20, 3.0))
+
+
+def plan(depth, chunks, start=5.0, own=0.8, delay=2.6, weights=WEIGHTS):
     per = 4.0 / chunks
     wire = {Q_RIGHT: 5.63 * per, Q_LEFT: 5.63 * per, STATE: 5.8 * per}
     wire.update({Y_QUERY: 2.82 * per, Y_PART: 2.9 * per})
-    work = {PICK: 0.15 * per, LOCAL: 0.6 * per, ACROSS: 0.6 * per, MERGE: 0.45 * per}
-    delay = 1.8
+    work = {PICK: 0.2, LOCAL: 0.45, ACROSS: 0.45, MERGE: 0.5}
     rank = {PICK: 0, ACROSS: 1, MERGE: 2, LOCAL: 3}
     events, tick = [], itertools.count()
     have = [set() for _ in range(depth)]
     queue, busy, last = {}, {}, {}
     idle = [False] * depth
     todo = [
-        {(kind, s, k) for kind in rank for s in range(depth) for k in range(chunks)}
-        for _ in range(depth)
+        {
+            (kind, s, k)
+            for kind in rank
+            for s in range(depth)
+            for k in range(chunks)
+            if kind != PICK or s != z
+        }
+        for z in range(depth)
     ]
     issued = [[] for _ in range(depth)]
 
@@ -59,7 +76,9 @@
         post(time + wire[op[0]] + delay, "land", tag, dest)
 
     def send(time, z, link, op, tag, dest):
-        order = (op[0] not in (Q_RIGHT, Q_LEFT, Y_QUERY), -abs(op[1] - z), op[2])
+        late = op[0] not in (Q_RIGHT, Q_LEFT, Y_QUERY)
+        a, b, c = weights[2 * (link == "y") + late]
+        order = a - b * abs(op[1] - z) + c * op[2]
         heapq.heappush(
             queue.setdefault((z, link), []), (order, next(tick), time, op, tag, dest)
         )
@@ -76,7 +95,7 @@
         if kind == PICK:
             return s == z or ("q", s, k) in have[z]
         if kind == LOCAL:
-            return (PICK, s, k) in have[z]
+            return s == z or (PICK, s, k) in have[z]
         if kind == ACROSS:
             return ("yq", s, k) in have[z]
         need = [(LOCAL, s, k), ("yp", s, k)]
@@ -94,19 +113,23 @@
         todo[z].remove(op)
         issued[z].append((time, 1, next(tick), op))
         idle[z] = False
-        if op[0] == PICK and op[1] != z:
+        if op[0] == PICK:
             send_query(time + 1e-3, z, op[1], op[2])
         post(time + work[op[0]], "done", z, op)
 
     for z in range(depth):
         for k in range(chunks):
             send_query(0.0, z, z, k)
+            post(own, "pick", z, k)
         post(start, "done", z, None)
     while events:
         time, _, what, facts = heapq.heappop(events)
         if what == "free":
             busy[facts[0]] = False
             pump(time, facts[0])
+        elif what == "pick":
+            z, k = facts
+            send(time, z, "y", (Y_QUERY, z, k), ("yq", z, k), z)
         elif what == "land":
             have[facts[1]].add(facts[0])
             turn(time, facts[1])
@@ -126,24 +149,37 @@
                     send(time, z, "left", (STATE, s, k), ("left", s, k), z - 1)
             turn(time, z)
     items = depth * chunks
+    early, early_y = EARLY, EARLY_Y
     orders = [
-        [op[0] * items + op[1] * chunks + op[2] for _, _, _, op in sorted(steps)]
-        for steps in issued
+        [
+            op[0] * items + op[1] * chunks + op[2]
+            for _, _, _, op in sorted(steps)
+            if not (op[0] in (Q_RIGHT, Q_LEFT) and op[1] == z and op[2] < early)
+            and not (op[0] == Y_QUERY and op[1] == z and op[2] < early_y)
+        ]
+        for z, steps in enumerate(issued)
     ]
     longest = max(len(o) for o in orders)
     return [o + [-1] * (longest - len(o)) for o in orders]
 
 
-def attend_part(query, keys, values, allowed):
-    scores = lax.dot_general(keys, query, NT, preferred_element_type=jnp.float32) * SCALE
-    scores = jnp.where(allowed, scores, NEG_BIG)
-    peak = jnp.max(scores, axis=0, keepdims=True)
-    expo = jnp.exp(scores - peak)
-    total = jnp.sum(expo, axis=0, keepdims=True)
-    out = lax.dot_general(
-        values, expo.astype(jnp.bfloat16), TN, preferred_element_type=jnp.float32
-    )
-    return out * (1.0 / total), peak + jnp.log(total)
+def attend_parts(queries, keys, values, allowed):
+    scores = [
+        lax.dot_general(k, q, NT, preferred_element_type=jnp.float32)
+        for q, k in zip(queries, keys)
+    ]
+    scores = [jnp.where(a, s, NEG_BIG) for s, a in zip(scores, allowed)]
+    peaks = [jnp.max(s, axis=0, keepdims=True) for s in scores]
+    expos = [jnp.exp2((s - p) * (SCALE * LOG2E)) for s, p in zip(scores, peaks)]
+    totals = [jnp.sum(e, axis=0, keepdims=True) for e in expos]
+    outs = [
+        lax.dot_general(
+            v, e.astype(jnp.bfloat16), TN, preferred_element_type=jnp.float32
+        )
+        for v, e in zip(values, expos)
+    ]
+    outs = [o * (1.0 / t) for o, t in zip(outs, totals)]
+    return outs, [p * SCALE + jnp.log(t) for p, t in zip(peaks, totals)]
 
 
 def chain(
@@ -247,6 +283,7 @@
     label_lane = lax.broadcasted_iota(jnp.int32, (n, HD), 1)
     told = jnp.zeros((n, HD), jnp.int32)
     owners, taken = [], []
+    asked = [jnp.int32(0)] * cap
     for p in range(reqs * slots):
         r, j = p // slots, p % slots
         count = jnp.clip(prefix[r] - j * page, 0, page)
@@ -257,52 +294,14 @@
             rank = rank + jnp.where(same, 1, 0)
         owners.append(owner)
         taken.append(jnp.where(count > 0, 1, 0))
+        beside = (owner == partner) & (count > 0)
+        asked = [jnp.where(beside & (rank == c), r, a) for c, a in enumerate(asked)]
         row = label_row == jnp.where(count > 0, owner, -1)
         facts = (table[r, j] - owner * pages_here, count, r, live[r])
         for f, fact in enumerate(facts):
             told = jnp.where(row & (label_lane == rank * 4 + f), fact, told)
     for d in range(depth):
         label_ref[d, 0:2, :] = told[2 * d : 2 * d + 2]
-
-    base, per_word = 9 * items + 1, 3
-    steps = len(orders[0])
-    words = []
-    for first in range(0, steps, per_word):
-        packed = [
-            sum((c + 1) * base**b for b, c in enumerate(o[first : first + per_word]))
-            for o in orders
-        ]
-        word = jnp.int32(packed[0])
-        for row in range(1, depth):
-            if packed[row] != packed[0]:
-                word = jnp.where(z == row, packed[row], word)
-        words.append(word)
-
-    def code_at(i):
-        at, b = i // per_word, i % per_word
-        word = words[0]
-        for w in range(1, len(words)):
-            word = jnp.where(at == w, words[w], word)
-        power = jnp.where(b == 0, 1, jnp.where(b == 1, base, base * base))
-        return (word // power) % base - 1
-
-    pl.semaphore_wait(barrier, n - 1)
-
-    def label_copy(d):
-        return pltpu.make_async_remote_copy(
-            src_ref=label_ref.at[d // 2],
-            dst_ref=labels.at[me],
-            send_sem=label_send_sem.at[d],
-            recv_sem=label_recv_sem.at[me],
-            device_id={"pages": d},
-            device_id_type=MESH,
-        )
-
-    def tell(i, _):
-        label_copy((me + i) % n).start()
-        return 0
-
-    lax.fori_loop(1, n, tell, 0)
 
     def q_copy(j, way):
         return pltpu.make_async_remote_copy(
@@ -368,30 +367,72 @@
                 device_id_type=MESH,
             ).wait_recv()
 
+    pl.semaphore_wait(barrier, n - 1)
+
+    def label_copy(d):
+        return pltpu.make_async_remote_copy(
+            src_ref=label_ref.at[d // 2],
+            dst_ref=labels.at[me],
+            send_sem=label_send_sem.at[d],
+            recv_sem=label_recv_sem.at[me],
+            device_id={"pages": d},
+            device_id_type=MESH,
+        )
+
+    def tell(i, _):
+        label_copy((me + i) % n).start()
+        return 0
+
+    lax.fori_loop(1, n, tell, 0)
+
     for copy in loads:
         copy.wait()
 
+    for k in range(EARLY):
+        j = z * chunks + k
+
+        @pl.when(z < depth - 1)
+        def _():
+            q_copy(j, 0).start()
+
+        @pl.when(z > 0)
+        def _():
+            q_copy(j, 1).start()
+
+    def own_pick(k, _):
+        j = z * chunks + k
+        q_now[...] = qa[j]
+        for c in range(cap):
+            yq_send[j, c] = q_now[asked[c]]
+
+        @pl.when(k < EARLY_Y)
+        def _():
+            yq_copy(j).start()
+
+        return 0
+
+    lax.fori_loop(0, chunks, own_pick, 0)
+
+    bits = (9 * items).bit_length()
+    per_word = 31 // bits
+    steps = -(-len(orders[0]) // per_word)
+    words = []
+    for w in range(steps):
+        packed = []
+        for o in orders:
+            few = o[w * per_word : (w + 1) * per_word]
+            few = few + [-1] * (per_word - len(few))
+            packed.append(
+                sum((9 * items if c < 0 else c) << (bits * b) for b, c in enumerate(few))
+            )
+        word = jnp.int32(packed[0])
+        for row in range(1, depth):
+            if packed[row] != packed[0]:
+                word = jnp.where(z == row, packed[row], word)
+        words.append(word)
+
     st_o[absent] = jnp.zeros_like(st_o[absent])
     st_s[absent] = jnp.full(st_s.shape[1:], NEG_BIG, jnp.float32)
-
-    def q_step(i, _):
-        code = code_at(i)
-        kind, j = code // items, code % items
-
-        @pl.when(kind == Q_RIGHT)
-        def _():
-            q_copy(j, 0).start()
-
-        @pl.when(kind == Q_LEFT)
-        def _():
-            q_copy(j, 1).start()
-
-        return 0
-
-    early = 0
-    while all(o[early] // items in (Q_RIGHT, Q_LEFT) for o in orders):
-        early += 1
-    lax.fori_loop(0, early, q_step, 0)
 
     def rows_of(query):
         return jnp.concatenate([query[:, head(h)] for h in range(heads)], axis=0)
@@ -425,15 +466,16 @@
     def tree_step(k, _):
         kv = k * heads // GROUPS
         lanes = pl.ds(pl.multiple_of(kv * HD, HD), HD)
-        for r in range(reqs):
-            out, lse = attend_part(
-                rows_of(qa[z * chunks + k, r]),
-                tk_ref[r, :, lanes],
-                tv_ref[r, :, lanes],
-                open_ref[r] > 0,
-            )
-            tree_o[k, r] = out
-            put_row(tree_s, k, r * tiles, lse)
+        every = range(reqs)
+        outs, lses = attend_parts(
+            [rows_of(qa[z * chunks + k, r]) for r in every],
+            [tk_ref[r, :, lanes] for r in every],
+            [tv_ref[r, :, lanes] for r in every],
+            [open_ref[r] > 0 for r in every],
+        )
+        for r in every:
+            tree_o[k, r] = outs[r]
+            put_row(tree_s, k, r * tiles, lses[r])
         return 0
 
     lax.fori_loop(0, chunks, tree_step, 0)
@@ -463,29 +505,26 @@
 
     def serve(d, k, query_of, out_ref, stat_ref, j):
         kv = k * heads // GROUPS
+        facts = [[label_now[d, y, c * 4 + f] for f in range(3)] for c in range(cap)]
+        outs, lses = attend_parts(
+            [rows_of(query_of(c, req)) for c, (_, _, req) in enumerate(facts)],
+            [pk_ref[kv, which] for which, _, _ in facts],
+            [pv_ref[kv, which] for which, _, _ in facts],
+            [key_row < count for _, count, _ in facts],
+        )
         for c in range(cap):
-            which, count, req = (label_now[d, y, c * 4 + f] for f in range(3))
-            out, lse = attend_part(
-                rows_of(query_of(c, req)),
-                pk_ref[kv, which],
-                pv_ref[kv, which],
-                key_row < count,
-            )
-            out_ref[j, c] = out.astype(jnp.bfloat16)
-            put_row(stat_ref, j, c * tiles, lse)
+            out_ref[j, c] = outs[c].astype(jnp.bfloat16)
+            put_row(stat_ref, j, c * tiles, lses[c])
 
     def pick(j, row, k):
-        @pl.when(row != z)
-        def _():
-            pltpu.make_async_remote_copy(
-                src_ref=qa.at[j],
-                dst_ref=qa.at[j],
-                send_sem=q_send_sem.at[0, j],
-                recv_sem=q_recv_sem.at[j],
-                device_id={"pages": partner},
-                device_id_type=MESH,
-            ).wait_recv()
-
+        pltpu.make_async_remote_copy(
+            src_ref=qa.at[j],
+            dst_ref=qa.at[j],
+            send_sem=q_send_sem.at[0, j],
+            recv_sem=q_recv_sem.at[j],
+            device_id={"pages": partner},
+            device_id_type=MESH,
+        ).wait_recv()
         q_now[...] = qa[j]
         for c in range(cap):
             yq_send[j, c] = q_now[label_now[row * 2 + y, 1 - y, c * 4 + 2]]
@@ -565,12 +604,12 @@
                     lanes = pl.ds(pl.multiple_of(k * wide + h * HD, HD), HD)
                     attended[r, :, lanes] = upright[h * tree : (h + 1) * tree]
 
-    def step(i, _):
-        code = code_at(i)
-        kind, j = code // items, code % items
-        row, k = j // chunks, j % chunks
-
-        @pl.when((kind >= 0) & (kind < Q_RIGHT))
+    def step(b, word):
+        code = (word >> (bits * b)) & ((1 << bits) - 1)
+        kind, j = split(code, items)
+        row, k = split(j, chunks)
+
+        @pl.when(kind < Q_RIGHT)
         def _():
             @pl.when(kind < ACROSS)
             def _():
@@ -618,9 +657,16 @@
                 yo_copy(j).start()
                 ys_copy(j).start()
 
-        return 0
-
-    lax.fori_loop(early, len(orders[0]), step, 0)
+        return word
+
+    def take(w, _):
+        word = words[0]
+        for i in range(1, steps):
+            word = jnp.where(w == i, words[i], word)
+        lax.fori_loop(0, per_word, step, word)
+        return 0
+
+    lax.fori_loop(0, steps, take, 0)
 
     page_row = lax.broadcasted_iota(jnp.int32, (pages_here, HD), 0)
 
@@ -668,7 +714,7 @@
     items = depth * chunks
     wide = width // chunks
     cols = wide // HD * tree
-    tall = max(8, max(reqs, cap) * cols // HD)
+    few, many = cap * cols // HD, reqs * cols // HD
     bf16, f32 = jnp.bfloat16, jnp.float32
     dma = pltpu.SemaphoreType.DMA
     smem = pl.BlockSpec(memory_space=pltpu.SMEM)
@@ -687,14 +733,14 @@
         ((items, cap, tree, wide), bf16),
         ((items, cap, HD, cols), bf16),
         ((items, cap, HD, cols), bf16),
-        ((items, tall, HD), f32),
-        ((items, tall, HD), f32),
+        ((items, few, HD), f32),
+        ((items, few, HD), f32),
         ((items, cap, HD, cols), bf16),
-        ((items, tall, HD), f32),
+        ((items, few, HD), f32),
         ((items + chunks + 1, reqs, HD, cols), bf16),
-        ((items + chunks + 1, tall, HD), f32),
+        ((items + chunks + 1, many, HD), f32),
         ((chunks, reqs, HD, cols), f32),
-        ((chunks, tall, HD), f32),
+        ((chunks, many, HD), f32),
         ((reqs, tree, cols), f32),
     ]
     scratch = [s and pltpu.VMEM(*s) for s in vmem_scratch]

time: 115 us -> 109 us (0.948)
  Pallas kernels: 110 us -> 105 us
    pallas_call x1, Pallas kernels: 110 us -> 105 us  [chain_call(): pl.pallas_call(functools.partial(chain, n, cap, chunks, orders), out_shap...]
where the time goes in v2:
time: 109 us
  Pallas kernels  105 us (96%)
  local copies, waits for them, and re-layouts  3.6 us (3%)
    pallas_call x1, Pallas kernels, chain_call(): pl.pallas_call(functools.partial(chain, n, cap, chunks, orders), out_shap...  105 us
    unnamed x1, local copies, waits for them, and re-layouts  2.3 us

profile of v2, /device:TPU:0, one launch (start us, length us, event | category | flops | bytes accessed | tf_op | source)
XLA Modules:
  0.0 108.9 jit_solution(14012770029195577355)
XLA Ops:
  0.6 104.6 %chain.1 = (bf16[4,64,2048]{2,1,0:T(8,128)(2,1)}, s32[8,128]{1,0:T(8,128)}) custom-call(s32[4,4]{1,0:T(4,128)} %table.1, s32[4]{0:T(128)} %prefix.1, s32[4]{0:T(128)} %live.1, s32[4,64]{1,0:T(4,128)} %parents_ref.1, bf16[4,64,512]{2,1,0:T(8,128)(2,1)} %tk_ref.1, bf16[4,64,512]{2,1,0:T(8,128)(2,1)} %tv_ref.1, bf16[4,64,2048]{2,1,0:T(8,128)(2,1)} %q_hbm.1, ...), custom_call_target="tpu_custom_call" | custom-call | tf_op jit(solution)/shard_map/chain/pallas_call | solution.py:765
  105.3 1.3 %slice_reduce_fusion = s32[8]{0:T(128)} fusion(s32[8,128]{1,0:T(8,128)} %get-tuple-element.5), kind=kLoop, calls=%fused_computation | loop fusion | bytes 64 | tf_op jit(solution)/shard_map/slice | solution.py:1222
  106.6 2.3 %copy.12 = bf16[4,64,2048]{2,1,0:T(8,128)(2,1)} copy(bf16[4,64,2048]{2,1,0:T(8,128)(2,1)} %get-tuple-element.8) | data formatting | bytes 2097152
